TPU v7x, 32 devices: a whole 2x2x4 slice. The times are simulated.
32 devices in a mesh: cand: 4 (over x, core), tp: 8 (over z, y).
Axes of the slice: x: 2, y: 2, z: 4, core: 2. Of those that a mesh axis runs over, the one named last changes fastest.
Arguments:
- start_state: float32 [128], replicated, may hold values from -6 to 6
- goal: float32 [128], replicated, may hold values from -6 to 6
- mean_prev: float32 [128], replicated, may hold values from -0.5 to 0.5
- std_prev: float32 [128], replicated, may hold values from 0.1 to 0.5
- noise: float32 [768, 128], P('cand'), may hold values from -23 to 23
- members: int32 [768, 1], P('cand'), may hold values from 0 to 3; in each aligned block of 192 rows (0 to 191, 192 to 383, ...) at most 60 rows name the same one
- elites: int32 [96], replicated, may hold values from 0 to 767, as said below
- w_in: bfloat16 [4, 144, 4096], P(None, None, 'tp'), may hold values from -0.5 to 0.5
- w_hid: bfloat16 [4, 4096, 4096], P(None, None, 'tp'), may hold values from -0.09375 to 0.09375
- w_out: bfloat16 [4, 4096, 128], P(None, 'tp'), may hold values from -0.09375 to 0.09375
Outputs:
- scores: float32 [768], P('cand')
- new_mean: float32 [128], replicated
- new_std: float32 [128], replicated
Inputs may be any that keep to these rules, and one draw needn't show every extreme that they name: `members`: among the candidates of one index of cand no member is named more than 60 times. `elites`: 96 distinct candidate numbers.
All inputs are finite; a program needn't handle non-finite values.
Results may differ from a plain program's by a relative error of at most 0.0085.
Values may be sent and summed in bfloat16 or wider, within the bound.
A program may use at most 64 MiB of HBM per device.

v0:
```python
import jax
import jax.numpy as jnp
from jax import lax
from jax.sharding import PartitionSpec as P

HORIZON = 8


def reward_of(states, goal, action):
    return -jnp.mean((states - goal) ** 2, axis=-1) - 0.1 * jnp.mean(action * action, axis=-1)


def on_device(start_state, goal, mean_prev, std_prev, noise, members, elites, w_in, w_hid, w_out):
    local_count = noise.shape[0]
    member_count = w_in.shape[0]
    state_width = start_state.shape[0]
    capacity = 5 * local_count // 16
    action_width = mean_prev.shape[0] // HORIZON
    actions = mean_prev[None, :] + std_prev[None, :] * noise
    onehot = (members == jnp.arange(member_count, dtype=jnp.int32)[None, :]).astype(jnp.float32)
    before = jnp.cumsum(onehot, axis=0) - onehot
    position = jnp.sum(before * onehot, axis=1).astype(jnp.int32)
    slot_number = members[:, 0] * capacity + position
    dispatch = (
        slot_number[None, :] == jnp.arange(member_count * capacity, dtype=jnp.int32)[:, None]
    ).astype(jnp.float32)
    slot_actions = jnp.dot(dispatch, actions, precision=lax.Precision.HIGHEST)
    slot_actions = slot_actions.reshape(member_count, capacity, HORIZON, action_width)
    input_layer = lax.all_gather(w_in, "tp", axis=2, tiled=True)

    def rollout(first, count):
        layer_in = input_layer[first : first + count]
        hid_rows = w_hid[first : first + count]
        out_rows = w_out[first : first + count]
        states = jnp.zeros((count, capacity, state_width), jnp.float32) + start_state[None, None, :]
        running = jnp.zeros((count, capacity), jnp.float32)
        for step_index in range(HORIZON):
            action = slot_actions[first : first + count, :, step_index, :]
            inputs = jnp.concatenate([states, action], axis=2).astype(jnp.bfloat16)
            first_pre = jnp.einsum(
                "mck,mkh->mch", inputs, layer_in, preferred_element_type=jnp.float32
            )
            hidden_one = jax.nn.silu(first_pre).astype(jnp.bfloat16)
            second_pre = jnp.einsum(
                "mck,mkh->mch", hidden_one, hid_rows, preferred_element_type=jnp.float32
            )
            hidden_two = jax.nn.silu(second_pre).astype(jnp.bfloat16)
            partial_change = jnp.einsum(
                "mck,mks->mcs", hidden_two, out_rows, preferred_element_type=jnp.float32
            )
            change = lax.psum(partial_change, "tp")
            states = states + change
            running = running + reward_of(states, goal[None, None, :], action)
        return running

    slot_returns = jnp.concatenate([rollout(member, 1) for member in range(member_count)], axis=0)
    returns = jnp.dot(
        slot_returns.reshape(member_count * capacity), dispatch, precision=lax.Precision.HIGHEST
    )
    first_index = lax.axis_index("cand") * local_count
    numbers = first_index + jnp.arange(local_count, dtype=jnp.int32)
    chosen = jnp.sum((elites[:, None] == numbers[None, :]).astype(jnp.float32), axis=0)
    count_all = local_count * lax.axis_size("cand")
    return_sum = lax.psum(jnp.sum(returns), "cand")
    return_mean = return_sum / count_all
    return_spread = lax.psum(jnp.sum((returns - return_mean) ** 2), "cand")
    return_var = return_spread / count_all
    scores = (returns - return_mean) / jnp.sqrt(return_var + 1e-06)
    weights = chosen * (0.5 + jax.nn.sigmoid(scores))
    weight_sum, first_moment = lax.psum(
        (jnp.sum(weights), jnp.dot(weights, actions, precision=lax.Precision.HIGHEST)), "cand"
    )
    new_mean = first_moment / weight_sum
    action_spread = lax.psum(
        jnp.dot(weights, (actions - new_mean[None, :]) ** 2, precision=lax.Precision.HIGHEST),
        "cand",
    )
    new_var = action_spread / weight_sum
    new_std = jnp.sqrt(new_var + 1e-06)
    return (scores, new_mean, new_std)


def solution(mesh):
    placed = (
        P(),
        P(),
        P(),
        P(),
        P("cand", None),
        P("cand", None),
        P(),
        P(None, None, "tp"),
        P(None, None, "tp"),
        P(None, "tp", None),
    )
    return jax.shard_map(
        on_device, mesh=mesh, in_specs=placed, out_specs=(P("cand"), P(), P()), check_vma=False
    )
```

profile of v0, /device:TPU:0, one launch (start us, length us, event | category | flops | bytes accessed | tf_op | source)
XLA Modules:
  0.0 847.4 jit_solution(5525363201203804489)
XLA Ops:
  16.0 77.4 %all-gather.2.cloned.1.call-done = bf16[4,144,4096]{2,1,0:T(8,128)(2,1)} async-done(((bf16[4,144,512]{2,1,0:T(8,128)(2,1)}), bf16[4,144,4096]{2,1,0:T(8,128)(2,1)}) %all-gather.2.cloned.1.call-update) | async-done | bytes 4718608 | tf_op jit(solution)/shard_map/all_gather | solution.py:29
  93.4 3.7 multiply_convert_fusion.109
  106.8 3.7 multiply_convert_fusion.85
  111.8 69.2 %all-reduce.33.cloned.1.call-done = (f32[1,60,128]{2,1,0:T(8,128)}, f32[1,60,128]{2,1,0:T(8,128)}, f32[1,60,128]{2,1,0:T(8,128)}, f32[1,60,128]{2,1,0:T(8,128)}) async-done(((f32[1,60,128]{2,1,0:T(8,128)}, f32[1,60,128]{2,1,0:T(8,128)}, f32[1,60,128]{2,1,0:T(8,128)}, f32[1,60,128]{2,1,0:T(8,128)}), (f32[1,60,128]{2,1,0:T(8,128)}, f32[1,60,128]{2,1,0:T(8,128)}, f32[1,60,128]{2,1,0:T(8,128)}, ...) | async-done | bytes 122896 | tf_op jit(solution)/shard_map/psum | solution.py:51
  195.1 3.7 multiply_convert_fusion.130
  200.4 69.7 %all-reduce.31.cloned.1.call-done = (f32[1,60,128]{2,1,0:T(8,128)}, f32[1,60,128]{2,1,0:T(8,128)}, f32[1,60,128]{2,1,0:T(8,128)}, f32[1,60,128]{2,1,0:T(8,128)}) async-done(((f32[1,60,128]{2,1,0:T(8,128)}, f32[1,60,128]{2,1,0:T(8,128)}, f32[1,60,128]{2,1,0:T(8,128)}, f32[1,60,128]{2,1,0:T(8,128)}), (f32[1,60,128]{2,1,0:T(8,128)}, f32[1,60,128]{2,1,0:T(8,128)}, f32[1,60,128]{2,1,0:T(8,128)}, ...) | async-done | bytes 122896 | tf_op jit(solution)/shard_map/psum | solution.py:51
  289.5 69.9 %all-reduce.29.cloned.1.call-done = (f32[1,60,128]{2,1,0:T(8,128)}, f32[1,60,128]{2,1,0:T(8,128)}, f32[1,60,128]{2,1,0:T(8,128)}, f32[1,60,128]{2,1,0:T(8,128)}) async-done(((f32[1,60,128]{2,1,0:T(8,128)}, f32[1,60,128]{2,1,0:T(8,128)}, f32[1,60,128]{2,1,0:T(8,128)}, f32[1,60,128]{2,1,0:T(8,128)}), (f32[1,60,128]{2,1,0:T(8,128)}, f32[1,60,128]{2,1,0:T(8,128)}, f32[1,60,128]{2,1,0:T(8,128)}, ...) | async-done | bytes 122896 | tf_op jit(solution)/shard_map/psum | solution.py:51
  360.2 3.7 multiply_convert_fusion.148
  373.6 3.7 multiply_convert_fusion.124
  378.8 69.9 %all-reduce.27.cloned.1.call-done = (f32[1,60,128]{2,1,0:T(8,128)}, f32[1,60,128]{2,1,0:T(8,128)}, f32[1,60,128]{2,1,0:T(8,128)}, f32[1,60,128]{2,1,0:T(8,128)}) async-done(((f32[1,60,128]{2,1,0:T(8,128)}, f32[1,60,128]{2,1,0:T(8,128)}, f32[1,60,128]{2,1,0:T(8,128)}, f32[1,60,128]{2,1,0:T(8,128)}), (f32[1,60,128]{2,1,0:T(8,128)}, f32[1,60,128]{2,1,0:T(8,128)}, f32[1,60,128]{2,1,0:T(8,128)}, ...) | async-done | bytes 122896 | tf_op jit(solution)/shard_map/psum | solution.py:51
  462.9 3.7 multiply_convert_fusion.121
  468.3 69.7 %all-reduce.25.cloned.1.call-done = (f32[1,60,128]{2,1,0:T(8,128)}, f32[1,60,128]{2,1,0:T(8,128)}, f32[1,60,128]{2,1,0:T(8,128)}, f32[1,60,128]{2,1,0:T(8,128)}) async-done(((f32[1,60,128]{2,1,0:T(8,128)}, f32[1,60,128]{2,1,0:T(8,128)}, f32[1,60,128]{2,1,0:T(8,128)}, f32[1,60,128]{2,1,0:T(8,128)}), (f32[1,60,128]{2,1,0:T(8,128)}, f32[1,60,128]{2,1,0:T(8,128)}, f32[1,60,128]{2,1,0:T(8,128)}, ...) | async-done | bytes 122896 | tf_op jit(solution)/shard_map/psum | solution.py:51
  538.7 3.7 multiply_convert_fusion.142
  543.2 3.7 multiply_convert_fusion.70
  557.2 70.0 %all-reduce.23.cloned.1.call-done = (f32[1,60,128]{2,1,0:T(8,128)}, f32[1,60,128]{2,1,0:T(8,128)}, f32[1,60,128]{2,1,0:T(8,128)}, f32[1,60,128]{2,1,0:T(8,128)}) async-done(((f32[1,60,128]{2,1,0:T(8,128)}, f32[1,60,128]{2,1,0:T(8,128)}, f32[1,60,128]{2,1,0:T(8,128)}, f32[1,60,128]{2,1,0:T(8,128)}), (f32[1,60,128]{2,1,0:T(8,128)}, f32[1,60,128]{2,1,0:T(8,128)}, f32[1,60,128]{2,1,0:T(8,128)}, ...) | async-done | bytes 122896 | tf_op jit(solution)/shard_map/psum | solution.py:51
  628.0 3.7 multiply_convert_fusion.139
  646.1 70.3 %all-reduce.21.cloned.1.call-done = (f32[1,60,128]{2,1,0:T(8,128)}, f32[1,60,128]{2,1,0:T(8,128)}, f32[1,60,128]{2,1,0:T(8,128)}, f32[1,60,128]{2,1,0:T(8,128)}) async-done(((f32[1,60,128]{2,1,0:T(8,128)}, f32[1,60,128]{2,1,0:T(8,128)}, f32[1,60,128]{2,1,0:T(8,128)}, f32[1,60,128]{2,1,0:T(8,128)}), (f32[1,60,128]{2,1,0:T(8,128)}, f32[1,60,128]{2,1,0:T(8,128)}, f32[1,60,128]{2,1,0:T(8,128)}, ...) | async-done | bytes 122896 | tf_op jit(solution)/shard_map/psum | solution.py:51
  721.7 3.7 multiply_convert_fusion.64
  730.7 3.7 multiply_convert_fusion.112
  735.2 70.5 %all-reduce.19.cloned.1.call-done = (f32[1,60,128]{2,1,0:T(8,128)}, f32[1,60,128]{2,1,0:T(8,128)}, f32[1,60,128]{2,1,0:T(8,128)}, f32[1,60,128]{2,1,0:T(8,128)}) async-done(((f32[1,60,128]{2,1,0:T(8,128)}, f32[1,60,128]{2,1,0:T(8,128)}, f32[1,60,128]{2,1,0:T(8,128)}, f32[1,60,128]{2,1,0:T(8,128)}), (f32[1,60,128]{2,1,0:T(8,128)}, f32[1,60,128]{2,1,0:T(8,128)}, f32[1,60,128]{2,1,0:T(8,128)}, ...) | async-done | bytes 122896 | tf_op jit(solution)/shard_map/psum | solution.py:51
  809.2 6.3 psum.291
  816.8 7.2 psum.292
  826.1 6.6 all-reduce.9
  833.6 6.0 psum.295
  (233 shorter events, 128.1 us)
Async XLA Ops:
  7.2 86.2 %all-gather.2.cloned.1.call-start = ((), (), s32[]{:S(2)}) async-start(), calls=%async_computation | async-start | bytes 5308416 | tf_op jit(solution)/shard_map/all_gather | solution.py:29
  7.9 173.0 %all-reduce.33.cloned.1.call-start = ((), (), s32[]{:S(2)}) async-start(), calls=%async_computation.8 | async-start | bytes 262144 | tf_op jit(solution)/shard_map/psum | solution.py:51
  106.8 74.1 %copy-start.22 = (f32[128]{0:T(128)S(1)}, f32[128]{0:T(128)}, u32[]{:S(2)}) copy-start(f32[128]{0:T(128)} %param.10) | copy-start | bytes 1540
  111.3 158.8 %all-reduce.31.cloned.1.call-start = ((), (), s32[]{:S(2)}) async-start(), calls=%async_computation.7 | async-start | bytes 262144 | tf_op jit(solution)/shard_map/psum | solution.py:51
  195.1 75.0 %copy-start.2 = (f32[1,60,128]{2,1,0:T(8,128)S(1)}, f32[1,60,128]{2,1,0:T(8,128)}, u32[]{:S(2)}) copy-start(f32[1,60,128]{2,1,0:T(8,128)} %get-tuple-element.73) | copy-start | bytes 92164
  195.1 75.0 %copy-start.3 = (f32[1,60,128]{2,1,0:T(8,128)S(1)}, f32[1,60,128]{2,1,0:T(8,128)}, u32[]{:S(2)}) copy-start(f32[1,60,128]{2,1,0:T(8,128)} %get-tuple-element.74) | copy-start | bytes 92164
  195.1 75.0 %copy-start.4 = (f32[1,60,128]{2,1,0:T(8,128)S(1)}, f32[1,60,128]{2,1,0:T(8,128)}, u32[]{:S(2)}) copy-start(f32[1,60,128]{2,1,0:T(8,128)} %get-tuple-element.75) | copy-start | bytes 92164
  195.1 75.0 %copy-start.5 = (f32[1,60,128]{2,1,0:T(8,128)S(1)}, f32[1,60,128]{2,1,0:T(8,128)}, u32[]{:S(2)}) copy-start(f32[1,60,128]{2,1,0:T(8,128)} %get-tuple-element.76) | copy-start | bytes 92164
  199.6 159.8 %all-reduce.29.cloned.1.call-start = ((), (), s32[]{:S(2)}) async-start(), calls=%async_computation.6 | async-start | bytes 262144 | tf_op jit(solution)/shard_map/psum | solution.py:51
  288.9 159.8 %all-reduce.27.cloned.1.call-start = ((), (), s32[]{:S(2)}) async-start(), calls=%async_computation.5 | async-start | bytes 262144 | tf_op jit(solution)/shard_map/psum | solution.py:51
  360.2 4.5 copy-start.12
  360.2 4.5 copy-start.13
  378.1 159.8 %all-reduce.25.cloned.1.call-start = ((), (), s32[]{:S(2)}) async-start(), calls=%async_computation.4 | async-start | bytes 262144 | tf_op jit(solution)/shard_map/psum | solution.py:51
  458.4 4.5 copy-start.8
  467.4 159.8 %all-reduce.23.cloned.1.call-start = ((), (), s32[]{:S(2)}) async-start(), calls=%async_computation.3 | async-start | bytes 262144 | tf_op jit(solution)/shard_map/psum | solution.py:51
  556.7 159.7 %all-reduce.21.cloned.1.call-start = ((), (), s32[]{:S(2)}) async-start(), calls=%async_computation.2 | async-start | bytes 262144 | tf_op jit(solution)/shard_map/psum | solution.py:51
  645.9 159.8 %all-reduce.19.cloned.1.call-start = ((), (), s32[]{:S(2)}) async-start(), calls=%async_computation.1 | async-start | bytes 262144 | tf_op jit(solution)/shard_map/psum | solution.py:51
  726.2 4.5 copy-start.14
  730.7 75.1 %copy-start.23 = (f32[128]{0:T(128)S(1)}, f32[128]{0:T(128)}, u32[]{:S(2)}) copy-start(f32[128]{0:T(128)} %param.11) | copy-start | bytes 1540
  730.7 86.1 %copy-start.25 = (s32[96]{0:T(128)S(1)}, s32[96]{0:T(128)}, u32[]{:S(2)}) copy-start(s32[96]{0:T(128)} %param.16) | copy-start | bytes 1156
  730.7 95.3 %copy-start.1 = (f32[192,128]{1,0:T(8,128)S(1)}, f32[192,128]{1,0:T(8,128)}, u32[]{:S(2)}) copy-start(f32[192,128]{1,0:T(8,128)} %param.14) | copy-start | bytes 294916
  730.7 95.2 %copy-start.20 = (f32[128]{0:T(128)S(1)}, f32[128]{0:T(128)}, u32[]{:S(2)}) copy-start(f32[128]{0:T(128)} %param.13) | copy-start | bytes 1540
  730.7 95.2 %copy-start.21 = (f32[128]{0:T(128)S(1)}, f32[128]{0:T(128)}, u32[]{:S(2)}) copy-start(f32[128]{0:T(128)} %param.12) | copy-start | bytes 1540
  833.4 7.4 copy-start.24
  (11 other events, 48.5 us)
Sparse Core Ops, SparseCore 0:
  10.0 83.3 all-gather.1
  111.4 69.4 all-reduce.32
  199.8 70.3 all-reduce.30
  289.0 70.3 all-reduce.28
  378.3 70.3 all-reduce.26
  467.5 70.4 all-reduce.24
  556.8 70.3 all-reduce.22
  646.1 70.3 all-reduce.20
  735.4 70.3 all-reduce.18
where the time goes:
time: 849 us; the launch traced here: 847 us
  waiting for transfers between devices  637 us (75%)
  matrix products  144 us (17%)
  blocking collectives  26.2 us (3%)
  other arithmetic  19 us (2%)
  between operations  15.8 us (2%)
    psum x8, waiting for transfers between devices, rollout(): change = lax.psum(partial_change, 'tp')  559 us
    dot_general x32, matrix products, rollout(): jnp.einsum('mck,mkh->mch', hidden_one, hid_rows, preferred_element_type=j...  118 us
    all_gather x1, waiting for transfers between devices, on_device(): input_layer = lax.all_gather(w_in, 'tp', axis=2, tiled=True)  77.4 us
    dot_general x32, matrix products, rollout(): jnp.einsum('mck,mks->mcs', hidden_two, out_rows, preferred_element_type=j...  24.4 us
  transfers between devices with their start and end apart: 9, of which 9 were waited for; matrix products, arithmetic and copies ran while one was open for 1% of the time, Pallas kernels for 0%

commit v1 on v0

--- a/solution.py
+++ b/solution.py
@@ -48,7 +48,8 @@
             partial_change = jnp.einsum(
                 "mck,mks->mcs", hidden_two, out_rows, preferred_element_type=jnp.float32
             )
-            change = lax.psum(partial_change, "tp")
+            parts = lax.all_gather(partial_change, "tp")
+            change = jnp.sum(parts, axis=0)
             states = states + change
             running = running + reward_of(states, goal[None, None, :], action)
         return running

time: 849 us -> 1260 us (1.48)
  blocking collectives: 26.2 us -> 1010 us
  waiting for transfers between devices: 637 us -> 76.1 us
  matrix products: 144 us -> 125 us
    all_gather x0 -> x32, blocking collectives: none -> 987 us  [rollout(): parts = lax.all_gather(partial_change, 'tp')]
    psum x8 -> x0, waiting for transfers between devices: 559 us -> none  [rollout(): change = lax.psum(partial_change, 'tp')]
    dot_general x32, matrix products: 24.4 us -> 4.88 us  [rollout(): jnp.einsum('mck,mks->mcs', hidden_two, out_rows, preferred_element_type=j...]
  transfers between devices with their start and end apart: 9 -> 1, of which waited for: 9 -> 1; matrix products, arithmetic and copies ran while one was open for 1% -> 1% of each run, Pallas kernels for 0% -> 0%
where the time goes in v1:
time: 1260 us; the launch traced here: 1250 us
  blocking collectives  1010 us (80%)
  matrix products  125 us (10%)
  waiting for transfers between devices  76.1 us (6%)
  between operations  16.4 us (1%)
    all_gather x32, blocking collectives, rollout(): parts = lax.all_gather(partial_change, 'tp')  987 us
    dot_general x32, matrix products, rollout(): jnp.einsum('mck,mkh->mch', hidden_one, hid_rows, preferred_element_type=j...  118 us
    all_gather x1, waiting for transfers between devices, on_device(): input_layer = lax.all_gather(w_in, 'tp', axis=2, tiled=True)  75.4 us
  transfers between devices with their start and end apart: 1, of which 1 were waited for; matrix products, arithmetic and copies ran while one was open for 1% of the time, Pallas kernels for 0%

profile of v1, /device:TPU:0, one launch (start us, length us, event | category | flops | bytes accessed | tf_op | source)
XLA Modules:
  0.0 1246.3 jit_solution(15353539271136131897)
XLA Ops:
  18.0 75.4 %all-gather.66.cloned.1.call-done = bf16[4,144,4096]{2,1,0:T(8,128)(2,1)} async-done(((bf16[4,144,512]{2,1,0:T(8,128)(2,1)}), bf16[4,144,4096]{2,1,0:T(8,128)(2,1)}) %all-gather.66.cloned.1.call-update) | async-done | bytes 4718608 | tf_op jit(solution)/shard_map/all_gather | solution.py:29
  108.9 30.9 %all-gather.40 = f32[8,60,128]{2,1,0:T(8,128)S(1)} all-gather(f32[1,60,128]{2,1,0:T(8,128)S(1)} %convolution_bitcast_fusion.23), channel_id=10, replica_groups=mesh['cand'=4,'tp'=8] {'tp'}, dimensions={0}, use_global_device_ids=true | all-gather | bytes 276480 | tf_op jit(solution)/shard_map/all_gather | solution.py:51
  139.8 31.0 %all-gather.32 = f32[8,60,128]{2,1,0:T(8,128)S(1)} all-gather(f32[1,60,128]{2,1,0:T(8,128)S(1)} %convolution_bitcast_fusion.31), channel_id=2, replica_groups=mesh['cand'=4,'tp'=8] {'tp'}, dimensions={0}, use_global_device_ids=true | all-gather | bytes 276480 | tf_op jit(solution)/shard_map/all_gather | solution.py:51
  178.6 31.1 %all-gather.33 = f32[8,60,128]{2,1,0:T(8,128)S(1)} all-gather(f32[1,60,128]{2,1,0:T(8,128)S(1)} %convolution_bitcast_fusion.30), channel_id=3, replica_groups=mesh['cand'=4,'tp'=8] {'tp'}, dimensions={0}, use_global_device_ids=true | all-gather | bytes 276480 | tf_op jit(solution)/shard_map/all_gather | solution.py:51
  209.7 31.0 %all-gather.41 = f32[8,60,128]{2,1,0:T(8,128)S(1)} all-gather(f32[1,60,128]{2,1,0:T(8,128)S(1)} %convolution_bitcast_fusion.22), channel_id=11, replica_groups=mesh['cand'=4,'tp'=8] {'tp'}, dimensions={0}, use_global_device_ids=true | all-gather | bytes 276480 | tf_op jit(solution)/shard_map/all_gather | solution.py:51
  240.7 31.0 %all-gather.56 = f32[8,60,128]{2,1,0:T(8,128)S(1)} all-gather(f32[1,60,128]{2,1,0:T(8,128)S(1)} %convolution_bitcast_fusion.7), channel_id=26, replica_groups=mesh['cand'=4,'tp'=8] {'tp'}, dimensions={0}, use_global_device_ids=true | all-gather | bytes 276480 | tf_op jit(solution)/shard_map/all_gather | solution.py:51
  271.7 30.8 %all-gather.48 = f32[8,60,128]{2,1,0:T(8,128)S(1)} all-gather(f32[1,60,128]{2,1,0:T(8,128)S(1)} %convolution_bitcast_fusion.15), channel_id=18, replica_groups=mesh['cand'=4,'tp'=8] {'tp'}, dimensions={0}, use_global_device_ids=true | all-gather | bytes 276480 | tf_op jit(solution)/shard_map/all_gather | solution.py:51
  314.1 31.2 %all-gather.34 = f32[8,60,128]{2,1,0:T(8,128)S(1)} all-gather(f32[1,60,128]{2,1,0:T(8,128)S(1)} %convolution_bitcast_fusion.29), channel_id=4, replica_groups=mesh['cand'=4,'tp'=8] {'tp'}, dimensions={0}, use_global_device_ids=true | all-gather | bytes 276480 | tf_op jit(solution)/shard_map/all_gather | solution.py:51
  349.3 30.9 %all-gather.35 = f32[8,60,128]{2,1,0:T(8,128)S(1)} all-gather(f32[1,60,128]{2,1,0:T(8,128)S(1)} %convolution_bitcast_fusion.28), channel_id=5, replica_groups=mesh['cand'=4,'tp'=8] {'tp'}, dimensions={0}, use_global_device_ids=true | all-gather | bytes 276480 | tf_op jit(solution)/shard_map/all_gather | solution.py:51
  384.1 30.9 %all-gather.36 = f32[8,60,128]{2,1,0:T(8,128)S(1)} all-gather(f32[1,60,128]{2,1,0:T(8,128)S(1)} %convolution_bitcast_fusion.27), channel_id=6, replica_groups=mesh['cand'=4,'tp'=8] {'tp'}, dimensions={0}, use_global_device_ids=true | all-gather | bytes 276480 | tf_op jit(solution)/shard_map/all_gather | solution.py:51
  418.9 30.9 %all-gather.37 = f32[8,60,128]{2,1,0:T(8,128)S(1)} all-gather(f32[1,60,128]{2,1,0:T(8,128)S(1)} %convolution_bitcast_fusion.26), channel_id=7, replica_groups=mesh['cand'=4,'tp'=8] {'tp'}, dimensions={0}, use_global_device_ids=true | all-gather | bytes 276480 | tf_op jit(solution)/shard_map/all_gather | solution.py:51
  453.7 30.9 %all-gather.38 = f32[8,60,128]{2,1,0:T(8,128)S(1)} all-gather(f32[1,60,128]{2,1,0:T(8,128)S(1)} %convolution_bitcast_fusion.25), channel_id=8, replica_groups=mesh['cand'=4,'tp'=8] {'tp'}, dimensions={0}, use_global_device_ids=true | all-gather | bytes 276480 | tf_op jit(solution)/shard_map/all_gather | solution.py:51
  488.5 30.8 %all-gather.39 = f32[8,60,128]{2,1,0:T(8,128)S(1)} all-gather(f32[1,60,128]{2,1,0:T(8,128)S(1)} %convolution_bitcast_fusion.24), channel_id=9, replica_groups=mesh['cand'=4,'tp'=8] {'tp'}, dimensions={0}, use_global_device_ids=true | all-gather | bytes 276480 | tf_op jit(solution)/shard_map/all_gather | solution.py:51
  519.3 30.8 %all-gather.49 = f32[8,60,128]{2,1,0:T(8,128)S(1)} all-gather(f32[1,60,128]{2,1,0:T(8,128)S(1)} %convolution_bitcast_fusion.14), channel_id=19, replica_groups=mesh['cand'=4,'tp'=8] {'tp'}, dimensions={0}, use_global_device_ids=true | all-gather | bytes 276480 | tf_op jit(solution)/shard_map/all_gather | solution.py:51
  550.1 30.8 %all-gather.42 = f32[8,60,128]{2,1,0:T(8,128)S(1)} all-gather(f32[1,60,128]{2,1,0:T(8,128)S(1)} %convolution_bitcast_fusion.21), channel_id=12, replica_groups=mesh['cand'=4,'tp'=8] {'tp'}, dimensions={0}, use_global_device_ids=true | all-gather | bytes 276480 | tf_op jit(solution)/shard_map/all_gather | solution.py:51
  584.8 30.8 %all-gather.43 = f32[8,60,128]{2,1,0:T(8,128)S(1)} all-gather(f32[1,60,128]{2,1,0:T(8,128)S(1)} %convolution_bitcast_fusion.20), channel_id=13, replica_groups=mesh['cand'=4,'tp'=8] {'tp'}, dimensions={0}, use_global_device_ids=true | all-gather | bytes 276480 | tf_op jit(solution)/shard_map/all_gather | solution.py:51
  654.1 31.0 %all-gather.45 = f32[8,60,128]{2,1,0:T(8,128)S(1)} all-gather(f32[1,60,128]{2,1,0:T(8,128)S(1)} %convolution_bitcast_fusion.18), channel_id=15, replica_groups=mesh['cand'=4,'tp'=8] {'tp'}, dimensions={0}, use_global_device_ids=true | all-gather | bytes 276480 | tf_op jit(solution)/shard_map/all_gather | solution.py:51
  697.2 30.8 %all-gather.57 = f32[8,60,128]{2,1,0:T(8,128)S(1)} all-gather(f32[1,60,128]{2,1,0:T(8,128)S(1)} %convolution_bitcast_fusion.6), channel_id=27, replica_groups=mesh['cand'=4,'tp'=8] {'tp'}, dimensions={0}, use_global_device_ids=true | all-gather | bytes 276480 | tf_op jit(solution)/shard_map/all_gather | solution.py:51
  731.9 30.8 %all-gather.58 = f32[8,60,128]{2,1,0:T(8,128)S(1)} all-gather(f32[1,60,128]{2,1,0:T(8,128)S(1)} %convolution_bitcast_fusion.5), channel_id=28, replica_groups=mesh['cand'=4,'tp'=8] {'tp'}, dimensions={0}, use_global_device_ids=true | all-gather | bytes 276480 | tf_op jit(solution)/shard_map/all_gather | solution.py:51
  835.8 30.9 %all-gather.61 = f32[8,60,128]{2,1,0:T(8,128)S(1)} all-gather(f32[1,60,128]{2,1,0:T(8,128)S(1)} %convolution_bitcast_fusion.2), channel_id=31, replica_groups=mesh['cand'=4,'tp'=8] {'tp'}, dimensions={0}, use_global_device_ids=true | all-gather | bytes 276480 | tf_op jit(solution)/shard_map/all_gather | solution.py:51
  870.6 30.9 %all-gather.62 = f32[8,60,128]{2,1,0:T(8,128)S(1)} all-gather(f32[1,60,128]{2,1,0:T(8,128)S(1)} %convolution_bitcast_fusion.1), channel_id=32, replica_groups=mesh['cand'=4,'tp'=8] {'tp'}, dimensions={0}, use_global_device_ids=true | all-gather | bytes 276480 | tf_op jit(solution)/shard_map/all_gather | solution.py:51
  936.2 30.8 %all-gather.50 = f32[8,60,128]{2,1,0:T(8,128)S(1)} all-gather(f32[1,60,128]{2,1,0:T(8,128)S(1)} %convolution_bitcast_fusion.13), channel_id=20, replica_groups=mesh['cand'=4,'tp'=8] {'tp'}, dimensions={0}, use_global_device_ids=true | all-gather | bytes 276480 | tf_op jit(solution)/shard_map/all_gather | solution.py:51
  970.9 30.9 %all-gather.51 = f32[8,60,128]{2,1,0:T(8,128)S(1)} all-gather(f32[1,60,128]{2,1,0:T(8,128)S(1)} %convolution_bitcast_fusion.12), channel_id=21, replica_groups=mesh['cand'=4,'tp'=8] {'tp'}, dimensions={0}, use_global_device_ids=true | all-gather | bytes 276480 | tf_op jit(solution)/shard_map/all_gather | solution.py:51
  1005.7 31.0 %all-gather.52 = f32[8,60,128]{2,1,0:T(8,128)S(1)} all-gather(f32[1,60,128]{2,1,0:T(8,128)S(1)} %convolution_bitcast_fusion.11), channel_id=22, replica_groups=mesh['cand'=4,'tp'=8] {'tp'}, dimensions={0}, use_global_device_ids=true | all-gather | bytes 276480 | tf_op jit(solution)/shard_map/all_gather | solution.py:51
  (222 shorter events, 443.6 us)
Async XLA Ops:
  7.2 86.2 %all-gather.66.cloned.1.call-start = ((), (), s32[]{:S(2)}) async-start(), calls=%async_computation | async-start | bytes 5308416 | tf_op jit(solution)/shard_map/all_gather | solution.py:29
  93.4 3.7 copy-start
  105.0 65.8 %copy-start.2 = (f32[128]{0:T(128)S(1)}, f32[128]{0:T(128)}, u32[]{:S(2)}) copy-start(f32[128]{0:T(128)} %param.10) | copy-start | bytes 1540
  650.3 34.9 %copy-start.5 = (f32[128]{0:T(128)S(1)}, f32[128]{0:T(128)}, u32[]{:S(2)}) copy-start(f32[128]{0:T(128)} %param.11) | copy-start | bytes 1540
  1171.3 43.6 %copy-start.7 = (s32[96]{0:T(128)S(1)}, s32[96]{0:T(128)}, u32[]{:S(2)}) copy-start(s32[96]{0:T(128)} %param.16) | copy-start | bytes 1156
  1171.4 53.0 %copy-start.1 = (f32[192,128]{1,0:T(8,128)S(1)}, f32[192,128]{1,0:T(8,128)}, u32[]{:S(2)}) copy-start(f32[192,128]{1,0:T(8,128)} %param.14) | copy-start | bytes 294916
  1171.4 53.0 %copy-start.3 = (f32[128]{0:T(128)S(1)}, f32[128]{0:T(128)}, u32[]{:S(2)}) copy-start(f32[128]{0:T(128)} %param.13) | copy-start | bytes 1540
  1171.4 53.0 %copy-start.4 = (f32[128]{0:T(128)S(1)}, f32[128]{0:T(128)}, u32[]{:S(2)}) copy-start(f32[128]{0:T(128)} %param.12) | copy-start | bytes 1540
  1231.8 7.4 copy-start.6
Sparse Core Ops, SparseCore 0:
  10.0 83.3 all-gather.65
